TPU v7x, 32 devices: a whole 2x2x4 slice. The times are simulated.
32 devices in a mesh: dp: 4 (over x, core), mp: 8 (over z, y).
Axes of the slice: x: 2, y: 2, z: 4, core: 2. Of those that a mesh axis runs over, the one named last changes fastest.
Arguments:
- tokens: bfloat16 [25088, 512], P(('dp', 'mp')), may hold values from -6 to 6
- cotangent: bfloat16 [25088, 512], P(('dp', 'mp')), may hold values from -6 to 6
- image_counts: int32 [4], replicated, may hold values from 1 to 32, 96 in all
- params: float32 [8, 394324], P('mp', 'dp'), may hold values from -4 to 4, as said below
- moment_one: float32 [8, 394324], P('mp', 'dp'), may hold values from -96 to 96
- moment_two: float32 [8, 394324], P('mp', 'dp'), may hold values from 0 to 40, as said below
Outputs:
- output: bfloat16 [25088, 512], P(('dp', 'mp'))
- input_grad: bfloat16 [25088, 512], P(('dp', 'mp'))
- param_grad: float32 [8, 394324], P('mp', 'dp')
- new_params: float32 [8, 394324], P('mp', 'dp')
- revised_first_mean: float32 [8, 394324], P('mp', 'dp')
- new_moment_two: float32 [8, 394324], P('mp', 'dp')
Inputs may be any that keep to these rules, and one draw needn't show every extreme that they name: `image_counts`: the live images of a group are its first slots; the counts add up to three quarters of all slots, rounded down, and one group is full. `params`: laid out as its meaning says. `moment_two`: Positive, laid out as params.
All inputs are finite; a program needn't handle non-finite values.
Results may differ from a plain program's by a relative error of at most 0.022.
Values may be sent and summed in bfloat16 or wider, within the bound.
A program may use at most 192 MiB of HBM per device.

v0:
```python
import math
import jax
import jax.numpy as jnp
from jax import lax
from jax.sharding import PartitionSpec as P

C = 512
FF = 2048
HD = 32
WIN = 7
MAP = 14
SHIFT = 3
norm_eps = 1e-05
mask_fill = -100.0
learn_rate = 0.05
beta_one = 0.9
second_decay_rate = 0.999
adam_eps = 1e-08
weight_decay = 0.05
adam_step = 2.0
small_labels = ["norm1_gain", "norm1_bias", "proj_bias", "norm2_gain", "norm2_bias", "fc2_bias"]


def combine_rule(spec, left, right):
    return jnp.einsum(spec, left, right, preferred_element_type=jnp.float32)


def contract_rows(left, right):
    return lax.dot_general(
        left, right, (((0,), (0,)), ((), ())), preferred_element_type=jnp.float32
    )


def contract_cols(left, right):
    return lax.dot_general(
        left, right, (((1,), (1,)), ((), ())), preferred_element_type=jnp.float32
    )


def segment_shapes(width_rank, hidden_rank):
    span = 2 * WIN - 1
    return [
        ("qkv_weight", (C, 3 * width_rank)),
        ("proj_weight", (width_rank, C)),
        ("fc1_weight", (C, hidden_rank)),
        ("fc2_weight", (hidden_rank, C)),
        ("norm1_gain", (width_rank,)),
        ("norm1_bias", (width_rank,)),
        ("query_bias", (width_rank,)),
        ("value_bias", (width_rank,)),
        ("proj_bias", (width_rank,)),
        ("norm2_gain", (width_rank,)),
        ("norm2_bias", (width_rank,)),
        ("fc1_bias", (hidden_rank,)),
        ("fc2_bias", (width_rank,)),
        ("table", (span * span, width_rank // HD)),
    ]


def unpack(flat, width_rank, hidden_rank):
    groups = flat.shape[0]
    owner_pieces = {}
    offset = 0
    for label, shape in segment_shapes(width_rank, hidden_rank):
        amount = math.prod(shape)
        owner_pieces[label] = flat[:, offset : offset + amount].reshape((groups,) + shape)
        offset = offset + amount
    return owner_pieces


def pack(owner_pieces, width_rank, hidden_rank, length):
    groups = owner_pieces["qkv_weight"].shape[0]
    parts = [
        owner_pieces[label].reshape(groups, -1)
        for label, shape in segment_shapes(width_rank, hidden_rank)
    ]
    used = sum((part.shape[1] for part in parts))
    parts.append(jnp.zeros((groups, length - used), jnp.float32))
    return jnp.concatenate(parts, axis=1)


def window_tables():
    side = MAP // WIN
    span = 2 * WIN - 1
    inner = jnp.arange(WIN * WIN, dtype=jnp.int32)
    row_in = inner // WIN
    col_in = inner % WIN
    offset_index = (row_in[:, None] - row_in[None, :] + WIN - 1) * span + (
        col_in[:, None] - col_in[None, :] + WIN - 1
    )
    one_hot = (
        offset_index.reshape(-1)[:, None] == jnp.arange(span * span, dtype=jnp.int32)[None, :]
    ).astype(jnp.float32)
    window_ids = jnp.arange(side * side, dtype=jnp.int32)
    row_coord = (window_ids // side)[:, None] * WIN + row_in[None, :]
    col_coord = (window_ids % side)[:, None] * WIN + col_in[None, :]

    def region(coord):
        return (coord >= MAP - WIN).astype(jnp.int32) + (coord >= MAP - SHIFT).astype(jnp.int32)

    region_ids = region(row_coord) * 3 + region(col_coord)
    mask = jnp.where(region_ids[:, :, None] == region_ids[:, None, :], 0.0, mask_fill).astype(
        jnp.float32
    )
    return (one_hot, mask)


def to_windows(raster):
    width = raster.shape[-1]
    side = MAP // WIN
    grid = raster.reshape(-1, MAP, MAP, width)
    grid = jnp.roll(grid, (-SHIFT, -SHIFT), (1, 2))
    grid = grid.reshape(-1, side, WIN, side, WIN, width).transpose(0, 1, 3, 2, 4, 5)
    return grid.reshape(-1, side * side, WIN * WIN, width)


def from_windows(blocks):
    width = blocks.shape[-1]
    side = MAP // WIN
    grid = blocks.reshape(-1, side, side, WIN, WIN, width).transpose(0, 1, 3, 2, 4, 5)
    grid = grid.reshape(-1, MAP, MAP, width)
    grid = jnp.roll(grid, (SHIFT, SHIFT), (1, 2))
    return grid.reshape(-1, width)


def norm_stats(values):
    center = jnp.mean(values, axis=1, keepdims=True)
    spread = jnp.mean(jnp.square(values - center), axis=1, keepdims=True)
    return (center, lax.rsqrt(spread + norm_eps))


def norm_back(scaled, unit, scale):
    return scale * (
        scaled
        - jnp.mean(scaled, axis=1, keepdims=True)
        - unit * jnp.mean(scaled * unit, axis=1, keepdims=True)
    )


def gelu(values):
    return values * (0.5 * (1.0 + lax.erf(values * (1.0 / math.sqrt(2.0)))))


def gelu_derivative(values):
    cdf = 0.5 * (1.0 + lax.erf(values * (1.0 / math.sqrt(2.0))))
    density = jnp.exp(-0.5 * values * values) * (1.0 / math.sqrt(2.0 * math.pi))
    return cdf + values * density


def qkv_finish(raw, query_bias, value_bias):
    shift = jnp.stack([query_bias, jnp.zeros_like(query_bias), value_bias], axis=1)
    factor = jnp.array([HD ** (-0.5), 1.0, 1.0], jnp.float32)[None, None, :, None]
    return ((raw + shift[None]) * factor).astype(jnp.bfloat16)


def window_scores(blocks, table, one_hot, mask):
    heads = table.shape[1]
    size = WIN * WIN
    bias = (
        jnp.dot(one_hot, table, precision=lax.Precision.HIGHEST)
        .reshape(size, size, heads)
        .transpose(2, 0, 1)
    )
    scores = combine_rule("nwphd,nwqhd->nwhpq", blocks[:, :, :, :, 0, :], blocks[:, :, :, :, 1, :])
    return scores + bias[None, None] + mask[None, :, None]


def attend_forward(projected, table, one_hot, mask):
    heads = table.shape[1]
    blocks = to_windows(projected)
    count, wins = (blocks.shape[0], blocks.shape[1])
    blocks = blocks.reshape(count, wins, WIN * WIN, heads, 3, HD)
    scores = window_scores(blocks, table, one_hot, mask)
    top = jnp.max(scores, axis=-1, keepdims=True)
    log_total = top + jnp.log(jnp.sum(jnp.exp(scores - top), axis=-1, keepdims=True))
    soft = jnp.exp(scores - log_total).astype(jnp.bfloat16)
    mixed = combine_rule("nwhpq,nwqhd->nwphd", soft, blocks[:, :, :, :, 2, :]).astype(jnp.bfloat16)
    return (from_windows(mixed.reshape(count, wins, WIN * WIN, heads * HD)), log_total)


def attend_backward(projected, grad_mixed, table, log_total, one_hot, mask):
    heads = table.shape[1]
    size = WIN * WIN
    blocks = to_windows(projected)
    count, wins = (blocks.shape[0], blocks.shape[1])
    blocks = blocks.reshape(count, wins, size, heads, 3, HD)
    scores = window_scores(blocks, table, one_hot, mask)
    soft = jnp.exp(scores - log_total)
    incoming = to_windows(grad_mixed).reshape(count, wins, size, heads, HD)
    grad_value = combine_rule("nwhpq,nwphd->nwqhd", soft.astype(jnp.bfloat16), incoming)
    grad_soft = combine_rule("nwphd,nwqhd->nwhpq", incoming, blocks[:, :, :, :, 2, :])
    inner = jnp.sum(soft * grad_soft, axis=-1, keepdims=True)
    grad_scores = soft * (grad_soft - inner)
    grad_bias = jnp.sum(grad_scores, axis=(0, 1)).transpose(1, 2, 0).reshape(size * size, heads)
    grad_table = jnp.dot(one_hot.T, grad_bias, precision=lax.Precision.HIGHEST)
    rounded = grad_scores.astype(jnp.bfloat16)
    grad_query = combine_rule("nwhpq,nwqhd->nwphd", rounded, blocks[:, :, :, :, 1, :]) * HD ** (
        -0.5
    )
    grad_key = combine_rule("nwhpq,nwphd->nwqhd", rounded, blocks[:, :, :, :, 0, :])
    stacked = jnp.stack([grad_query, grad_key, grad_value], axis=4).reshape(
        count, wins, size, heads * 3 * HD
    )
    return (from_windows(stacked), grad_table)


def head_block(tokens, cotangent, live, live_all, owner_pieces, rank, one_hot, mask):
    ranks = lax.axis_size("mp")
    width_rank = owner_pieces["proj_weight"].shape[1]
    heads = width_rank // HD
    rows = tokens.shape[0]

    def linear_entries_arg(label):
        return owner_pieces[label][0].astype(jnp.float32)

    live_col = live[:, None]
    smalls = jnp.stack([owner_pieces[label][0] for label in small_labels])
    whole, cot_all, smalls_all = (
        lax.all_gather(tokens, "mp", axis=0, tiled=True),
        lax.all_gather(cotangent, "mp", axis=0, tiled=True),
        lax.all_gather(smalls, "mp", axis=1, tiled=True),
    )
    full = smalls_all.astype(jnp.float32)
    inputs_all = whole.astype(jnp.float32)
    center1, scale1 = norm_stats(inputs_all)
    unit1 = (inputs_all - center1) * scale1
    normed1 = (unit1 * full[0] + full[1]).astype(jnp.bfloat16)
    group_rows = whole.shape[0]
    raw = jnp.dot(
        normed1, owner_pieces["qkv_weight"][0], preferred_element_type=jnp.float32
    ).reshape(group_rows, heads, 3, HD)
    projected = qkv_finish(
        raw,
        linear_entries_arg("query_bias").reshape(heads, HD),
        linear_entries_arg("value_bias").reshape(heads, HD),
    )
    projected = projected.reshape(group_rows, heads * 3 * HD)
    table = owner_pieces["table"][0].astype(jnp.float32)
    mixed, log_total = attend_forward(projected, table, one_hot, mask)
    partial_value = jnp.dot(
        mixed, owner_pieces["proj_weight"][0], preferred_element_type=jnp.float32
    )
    attended = (
        lax.psum_scatter(
            partial_value.astype(jnp.bfloat16), "mp", scatter_dimension=0, tiled=True
        ).astype(jnp.float32)
        + full[2]
    )
    inputs = tokens.astype(jnp.float32)
    residual = inputs + attended
    center2, scale2 = norm_stats(residual)
    unit2 = (residual - center2) * scale2
    normed2 = (unit2 * full[3] + full[4]).astype(jnp.bfloat16)
    normed2_all = lax.all_gather(normed2, "mp", axis=0, tiled=True)
    hidden_before_gelu = jnp.dot(
        normed2_all, owner_pieces["fc1_weight"][0], preferred_element_type=jnp.float32
    ) + linear_entries_arg("fc1_bias")
    nonlinear_token_list = gelu(hidden_before_gelu).astype(jnp.bfloat16)
    feed_part = jnp.dot(
        nonlinear_token_list, owner_pieces["fc2_weight"][0], preferred_element_type=jnp.float32
    )
    perceptron_result = (
        lax.psum_scatter(
            feed_part.astype(jnp.bfloat16), "mp", scatter_dimension=0, tiled=True
        ).astype(jnp.float32)
        + full[5]
    )
    output = (live_col * (residual + perceptron_result)).astype(jnp.bfloat16)
    grad_out = live_col * cotangent.astype(jnp.float32)
    parameter_gradients = {}
    grad_all = cot_all * live_all[:, None].astype(jnp.bfloat16)
    parameter_gradients["fc2_weight"] = contract_rows(nonlinear_token_list, grad_all)[None]
    gradient_before_gelu = contract_cols(grad_all, owner_pieces["fc2_weight"][0]) * gelu_derivative(
        hidden_before_gelu
    )
    parameter_gradients["fc1_bias"] = jnp.sum(gradient_before_gelu, axis=0)[None]
    preact_rounded = gradient_before_gelu.astype(jnp.bfloat16)
    parameter_gradients["fc1_weight"] = contract_rows(normed2_all, preact_rounded)[None]
    grad_norm2 = lax.psum_scatter(
        contract_cols(preact_rounded, owner_pieces["fc1_weight"][0]).astype(jnp.bfloat16),
        "mp",
        scatter_dimension=0,
        tiled=True,
    ).astype(jnp.float32)
    grad_residual = grad_out + norm_back(grad_norm2 * full[3], unit2, scale2)
    residual_rounded = grad_residual.astype(jnp.bfloat16)
    rounded_all = lax.all_gather(residual_rounded, "mp", axis=0, tiled=True)
    parameter_gradients["proj_weight"] = contract_rows(mixed, rounded_all)[None]
    grad_mixed = contract_cols(rounded_all, owner_pieces["proj_weight"][0]).astype(jnp.bfloat16)
    grad_projected, grad_table = attend_backward(
        projected, grad_mixed, table, log_total, one_hot, mask
    )
    split = grad_projected.reshape(group_rows, heads, 3, HD)
    parameter_gradients["query_bias"] = jnp.sum(split[:, :, 0, :], axis=0).reshape(1, width_rank)
    parameter_gradients["value_bias"] = jnp.sum(split[:, :, 2, :], axis=0).reshape(1, width_rank)
    parameter_gradients["table"] = grad_table[None]
    projected_rounded = grad_projected.astype(jnp.bfloat16)
    parameter_gradients["qkv_weight"] = contract_rows(normed1, projected_rounded)[None]
    norm1_part = contract_cols(projected_rounded, owner_pieces["qkv_weight"][0])
    grad_norm1 = lax.psum_scatter(
        norm1_part.astype(jnp.bfloat16), "mp", scatter_dimension=0, tiled=True
    ).astype(jnp.float32)
    unit1_own = lax.dynamic_slice_in_dim(unit1, rank * rows, rows, 0)
    scale1_own = lax.dynamic_slice_in_dim(scale1, rank * rows, rows, 0)
    grad_input = (grad_residual + norm_back(grad_norm1 * full[0], unit1_own, scale1_own)).astype(
        jnp.bfloat16
    )
    small_terms = jnp.stack(
        [
            jnp.sum(grad_norm1 * unit1_own, axis=0),
            jnp.sum(grad_norm1, axis=0),
            jnp.sum(grad_residual, axis=0),
            jnp.sum(grad_norm2 * unit2, axis=0),
            jnp.sum(grad_norm2, axis=0),
            jnp.sum(grad_out, axis=0),
        ]
    ).reshape(len(small_labels), ranks, width_rank)
    small_sums = lax.psum_scatter(small_terms, "mp", scatter_dimension=1, tiled=True)
    for index, label in enumerate(small_labels):
        parameter_gradients[label] = small_sums[index]
    return (output, grad_input, parameter_gradients)


def local(tokens, cotangent, image_counts, params, moment_one, moment_two):
    ranks = lax.axis_size("mp")
    rank = lax.axis_index("mp")
    group = lax.axis_index("dp")
    width_rank = C // ranks
    hidden_rank = FF // ranks
    pixels = MAP * MAP
    rows = tokens.shape[0]
    shard_length = params.shape[1]
    one_hot, mask = window_tables()
    owned = lax.all_gather(params.astype(jnp.bfloat16), "dp", axis=1, tiled=True)
    limit = jnp.sum(
        jnp.where(jnp.arange(image_counts.shape[0], dtype=jnp.int32) == group, image_counts, 0)
    )
    images = rank * (rows // pixels) + jnp.arange(rows, dtype=jnp.int32) // pixels
    live = (images < limit).astype(jnp.float32)
    owner_pieces = unpack(owned, width_rank, hidden_rank)
    live_all = (jnp.arange(rows * ranks, dtype=jnp.int32) // pixels < limit).astype(jnp.float32)
    output, grad_input, parameter_gradients = head_block(
        tokens, cotangent, live, live_all, owner_pieces, rank, one_hot, mask
    )
    flat = pack(parameter_gradients, width_rank, hidden_rank, owned.shape[1])
    grad_shard = lax.psum_scatter(flat, "dp", scatter_dimension=1, tiled=True)
    weights_rank = (4 * C * C + 2 * C * FF) // ranks
    position = group * shard_length + jnp.arange(shard_length, dtype=jnp.int32)[None, :]
    decays = (position < weights_rank).astype(jnp.float32)
    new_one = beta_one * moment_one + (1.0 - beta_one) * grad_shard
    new_two = second_decay_rate * moment_two + (1.0 - second_decay_rate) * grad_shard * grad_shard
    corrected_one = new_one / (1.0 - beta_one**adam_step)
    corrected_two = new_two / (1.0 - second_decay_rate**adam_step)
    new_params = params - learn_rate * (
        corrected_one / (jnp.sqrt(corrected_two) + adam_eps) + weight_decay * decays * params
    )
    return (output, grad_input, grad_shard, new_params, new_one, new_two)


def solution(mesh):
    return jax.shard_map(
        local,
        mesh=mesh,
        in_specs=(
            P(("dp", "mp"), None),
            P(("dp", "mp"), None),
            P(),
            P("mp", "dp"),
            P("mp", "dp"),
            P("mp", "dp"),
        ),
        out_specs=(
            P(("dp", "mp"), None),
            P(("dp", "mp"), None),
            P("mp", "dp"),
            P("mp", "dp"),
            P("mp", "dp"),
            P("mp", "dp"),
        ),
        check_vma=False,
    )
```

profile of v0, /device:TPU:0, one launch (start us, length us, event | category | flops | bytes accessed | tf_op | source)
XLA Modules:
  0.0 1341.9 jit_solution(6521785367379511616)
XLA Ops:
  8.1 2.0 convert_reduce_fusion.3
  12.2 2.1 dynamic-update-slice
  16.2 36.5 %all-reduce.6.cloned.1.call-done = bf16[394324]{0:T(1024)(128)(2,1)} async-done(((bf16[394324]{0:T(1024)(128)(2,1)}), bf16[394324]{0:T(1024)(128)(2,1)}) %all-reduce.6.cloned.1.call-update) | async-done | bytes 788664
  52.7 8.4 reshape.473
  61.5 27.7 %all-gather = bf16[8,64,6]{1,2,0:T(8,128)(2,1)S(1)} all-gather(bf16[1,64,6]{1,2,0:T(8,128)(2,1)S(1)} %bitcast.187), channel_id=1, replica_groups=mesh['dp'=4,'mp'=8] {'mp'}, dimensions={0}, use_global_device_ids=true | all-gather | bytes 6912 | tf_op jit(solution)/shard_map/all_gather | solution.py:221
  93.6 27.4 %all-gather.6.cloned.1.call-done = bf16[6272,512]{1,0:T(8,128)(2,1)} async-done(((bf16[784,512]{1,0:T(8,128)(2,1)}), bf16[6272,512]{1,0:T(8,128)(2,1)}) %all-gather.6.cloned.1.call-update) | async-done | bytes 6422544 | tf_op jit(solution)/shard_map/all_gather | solution.py:219
  121.0 3.9 convert_reduce_fusion
  125.7 2.9 fusion.2
  128.7 5.7 fusion.4
  134.4 12.6 copy.83
  147.0 21.8 %reshape_reshape.20 = bf16[32,14,14,192]{3,2,1,0:T(8,128)(2,1)} reshape(bf16[6272,2,3,32]{3,2,1,0:T(4,128)(2,1)} %copy.83) | data formatting | bytes 4816896 | tf_op jit(solution)/shard_map/reshape;reshape | solution.py:111
  177.0 11.2 reshape_reshape.21
  188.2 25.3 %fusion.105 = (bf16[32,4,49,2,1,32]{5,4,3,0,2,1:T(2,128)(2,1)}, bf16[32,4,49,2,1,32]{5,4,3,0,2,1:T(2,128)(2,1)}, bf16[32,4,49,2,1,32]{5,4,3,0,2,1:T(2,128)(2,1)}) fusion(bf16[32,4,49,2,3,32]{5,4,3,0,2,1:T(4,128)(2,1)} %reshape_reshape.21), kind=kLoop, calls=%fused_computation.208 | loop fusion | bytes 4816896 | tf_op jit(solution)/shard_map/slice | solution.py:164
  213.5 12.7 copy.124
  226.3 14.0 %copy.123 = bf16[32,4,49,2,1,32]{2,5,3,1,0,4:T(8,128)(2,1)} copy(bf16[32,4,49,2,1,32]{5,4,3,0,2,1:T(2,128)(2,1)} %get-tuple-element.29) | data formatting | bytes 1605632
  240.3 13.9 %copy.125 = bf16[32,4,49,2,1,32]{2,5,3,1,0,4:T(8,128)(2,1)} copy(bf16[32,4,49,2,1,32]{5,4,3,0,2,1:T(2,128)(2,1)} %get-tuple-element.30) | data formatting | bytes 1605632
  254.2 3.8 fusion.14
  258.1 2.6 exponential_reduce_fusion
  261.4 3.3 convert_bitcast_fusion
  264.7 7.8 copy.92
  272.5 2.6 reshape_reshape.22
  280.2 5.4 convolution_convert_fusion.3
  286.2 117.6 %reduce-scatter.7.cloned.1.call-done = bf16[784,512]{1,0:T(8,128)(2,1)} async-done(((bf16[6272,512]{1,0:T(8,128)(2,1)}), bf16[784,512]{1,0:T(8,128)(2,1)}) %reduce-scatter.7.cloned.1.call-update) | async-done | bytes 802832 | tf_op jit(solution)/shard_map/reduce_scatter | solution.py:244
  410.5 3.0 slice_reduce_fusion.2
  414.5 93.3 %all-gather.8.cloned.1.call-done = bf16[6272,512]{1,0:T(8,128)(2,1)} async-done(((bf16[784,512]{1,0:T(8,128)(2,1)}), bf16[6272,512]{1,0:T(8,128)(2,1)}) %all-gather.8.cloned.1.call-update) | async-done | bytes 6422544 | tf_op jit(solution)/shard_map/all_gather | solution.py:254
  507.9 6.6 multiply_convert_fusion
  514.5 93.9 %all-gather.10.cloned.1.call-done = bf16[6272,512]{1,0:T(8,128)(2,1)} async-done(((bf16[784,512]{1,0:T(8,128)(2,1)}), bf16[6272,512]{1,0:T(8,128)(2,1)}) %all-gather.10.cloned.1.call-update) | async-done | bytes 6422544 | tf_op jit(solution)/shard_map/all_gather | solution.py:220
  608.4 8.1 fusion.109
  616.5 4.5 convolution_convert_fusion.1
  621.1 6.5 convolution_convert_fusion.2
  628.5 110.6 %reduce-scatter.11.cloned.1.call-done = bf16[784,512]{1,0:T(8,128)(2,1)} async-done(((bf16[6272,512]{1,0:T(8,128)(2,1)}), bf16[784,512]{1,0:T(8,128)(2,1)}) %reduce-scatter.11.cloned.1.call-update) | async-done | bytes 802832 | tf_op jit(solution)/shard_map/reduce_scatter | solution.py:279
  739.1 2.7 fusion.53
  741.8 120.0 %reduce-scatter.9.cloned.1.call-done = bf16[784,512]{1,0:T(8,128)(2,1)} async-done(((bf16[6272,512]{1,0:T(8,128)(2,1)}), bf16[784,512]{1,0:T(8,128)(2,1)}) %reduce-scatter.9.cloned.1.call-update) | async-done | bytes 802832 | tf_op jit(solution)/shard_map/reduce_scatter | solution.py:263
  861.8 3.6 fusion.103
  869.0 9.1 fusion
  878.1 4.9 fusion.61
  884.3 5.1 fusion.64
  893.4 73.7 %all-gather.12.cloned.1.call-done = bf16[6272,512]{1,0:T(8,128)(2,1)} async-done(((bf16[784,512]{1,0:T(8,128)(2,1)}), bf16[6272,512]{1,0:T(8,128)(2,1)}) %all-gather.12.cloned.1.call-update) | async-done | bytes 6422544 | tf_op jit(solution)/shard_map/all_gather | solution.py:287
  967.1 4.9 convolution_convert_fusion.4
  976.3 2.9 reshape_reshape.23
  979.2 8.8 copy.98
  988.1 7.9 convolution_bitcast_fusion
  996.0 3.2 multiply_reduce_fusion
  999.3 2.8 fusion.102
  1002.0 4.0 convolution_bitcast_fusion.1
  1006.0 3.2 multiply_bitcast_fusion
  1009.2 10.6 pad_maximum_fusion
  1019.8 23.6 %copy.103 = f32[32,4,49,2,3,32]{5,4,3,0,2,1:T(4,128)} copy(f32[32,4,49,2,3,32]{2,5,3,1,0,4:T(8,128)} %pad_maximum_fusion) | data formatting | bytes 9633792 | tf_op jit(solution)/shard_map/stack | solution.py:201
  1043.3 26.9 %reshape_reshape.24 = f32[32,2,2,7,7,192]{5,0,4,3,2,1:T(8,128)} reshape(f32[32,4,49,2,3,32]{5,4,3,0,2,1:T(4,128)} %copy.103) | data formatting | bytes 9633792 | tf_op jit(solution)/shard_map/reshape;reshape | solution.py:120
  1070.2 3.4 copy.104
  1074.9 3.7 fusion.9
  1084.6 3.7 copy.105
  1088.2 5.1 convert_element_type.224
  1093.4 4.6 convolution_convert_fusion
  1097.9 8.5 fusion.43
  1108.0 9.5 copy.107
  1117.6 24.9 %reshape_reshape.25 = f32[6272,2,3,32]{3,2,1,0:T(4,128)} reshape(f32[32,14,14,192]{3,2,1,0:T(8,128)} %copy.107) | data formatting | bytes 9633792 | tf_op jit(solution)/shard_map/reshape;reshape | solution.py:293
  1142.5 25.9 %slice_reduce_fusion = (f32[2,32]{1,0:T(2,128)S(1)}, f32[2,32]{1,0:T(2,128)S(1)}) fusion(f32[6272,2,3,32]{3,2,1,0:T(4,128)} %reshape_reshape.25), kind=kLoop, calls=%fused_computation.27 | loop fusion | flops 802688 | bytes 3211776 | tf_op jit(solution)/shard_map/reduce_sum | solution.py:295
  1172.1 63.5 %reduce-scatter.13.cloned.1.call-done = bf16[784,512]{1,0:T(8,128)(2,1)} async-done(((bf16[6272,512]{1,0:T(8,128)(2,1)}), bf16[784,512]{1,0:T(8,128)(2,1)}) %reduce-scatter.13.cloned.1.call-update) | async-done | bytes 802832 | tf_op jit(solution)/shard_map/reduce_scatter | solution.py:300
  1235.7 2.3 fusion.54
  1238.2 35.5 %all-reduce.1 = f32[6,8,64]{2,1,0:T(8,128)S(1)} all-reduce(f32[6,8,64]{2,1,0:T(8,128)S(1)} %constant_dynamic-update-slice_fusion), channel_id=6, replica_groups=mesh['dp'=4,'mp'=8] {'mp'}, use_global_device_ids=true, to_apply=%region_22.23.clone | all-reduce | flops 3072 | bytes 24576
  1289.5 2.8 fusion.47
  1292.3 37.1 %all-reduce.8.cloned.1.call-done = f32[1,394324]{1,0:T(1,128)} async-done(((f32[1,394324]{1,0:T(1,128)}), f32[1,394324]{1,0:T(1,128)}) %all-reduce.8.cloned.1.call-update) | async-done | bytes 1577312
  1329.4 4.9 multiply_subtract_fusion
  (258 shorter events, 73.0 us)
Async XLA Ops:
  8.0 44.7 %all-reduce.6.cloned.1.call-start = ((), (), s32[]{:S(2)}) async-start(), calls=%async_computation.12 | async-start | bytes 1581056
  15.2 105.8 %all-gather.6.cloned.1.call-start = ((), (), s32[]{:S(2)}) async-start(), calls=%async_computation.4 | async-start | bytes 7225344 | tf_op jit(solution)/shard_map/all_gather | solution.py:219
  15.8 388.0 %reduce-scatter.7.cloned.1.call-start = ((), (), s32[]{:S(2)}) async-start(), calls=%async_computation.5 | async-start | bytes 7225344 | tf_op jit(solution)/shard_map/reduce_scatter | solution.py:244
  16.1 75.5 %copy-start.39 = (s32[49,49]{1,0:T(8,128)}, s32[49,49]{1,0:T(8,128)S(1)}, u32[]{:S(2)}) copy-start(s32[49,49]{1,0:T(8,128)S(1)} %add_add_fusion.2) | copy-start | bytes 28816
  61.0 63.9 %copy-start.15 = (bf16[1,394324]{1,0:T(2,128)(2,1)}, bf16[1,394324]{1,0:T(2,128)(2,1)S(1)}, u32[]{:S(2)}) copy-start(bf16[1,394324]{1,0:T(2,128)(2,1)S(1)} %reshape.473) | copy-start | bytes 2365948
  90.5 170.2 %copy-start.22 = (f32[2,49,49]{1,2,0:T(8,128)}, f32[2,49,49]{1,2,0:T(8,128)S(1)}, u32[]{:S(2)}) copy-start(f32[2,49,49]{1,2,0:T(8,128)S(1)} %copy.90) | copy-start | bytes 57628
  92.9 35.7 %copy-start.25 = (bf16[512,192]{1,0:T(8,128)(2,1)}, bf16[512,192]{1,0:T(8,128)(2,1)S(1)}, u32[]{:S(2)}) copy-start(bf16[512,192]{1,0:T(8,128)(2,1)S(1)} %squeeze_reshape.19) | copy-start | bytes 589828
  93.6 35.0 %copy-start.43 = (f32[1,512]{1,0:T(1,128)}, f32[1,512]{1,0:T(1,128)S(1)}, u32[]{:S(2)}) copy-start(f32[1,512]{1,0:T(1,128)S(1)} %get-tuple-element.50) | copy-start | bytes 6148
  93.6 35.0 %copy-start.52 = (f32[1,512]{1,0:T(1,128)}, f32[1,512]{1,0:T(1,128)S(1)}, u32[]{:S(2)}) copy-start(f32[1,512]{1,0:T(1,128)S(1)} %get-tuple-element.49) | copy-start | bytes 6148
  121.0 4.7 copy-start.1
  124.9 3.8 copy-start.57
  125.7 8.8 copy-start.33
  128.6 5.8 copy-start.36
  226.3 27.9 %copy-start.6 = (bf16[32,4,49,2,1,32]{2,5,3,1,0,4:T(8,128)(2,1)}, bf16[32,4,49,2,1,32]{2,5,3,1,0,4:T(8,128)(2,1)S(1)}, u32[]{:S(2)}) copy-start(bf16[32,4,49,2,1,32]{2,5,3,1,0,4:T(8,128)(2,1)S(1)} %copy.124) | copy-start | bytes 2408452
  258.1 3.3 copy-start.9
  285.6 118.1 %copy-start.2 = (bf16[784,512]{1,0:T(8,128)(2,1)S(1)}, bf16[784,512]{1,0:T(8,128)(2,1)}, u32[]{:S(2)}) copy-start(bf16[784,512]{1,0:T(8,128)(2,1)} %param.7) | copy-start | bytes 2408452
  285.6 118.1 %copy-start.41 = (f32[1,512]{1,0:T(1,128)S(1)}, f32[1,512]{1,0:T(1,128)}, u32[]{:S(2)}) copy-start(f32[1,512]{1,0:T(1,128)} %get-tuple-element.48) | copy-start | bytes 6148
  285.6 121.3 %copy-start.42 = (f32[1,512]{1,0:T(1,128)S(1)}, f32[1,512]{1,0:T(1,128)}, u32[]{:S(2)}) copy-start(f32[1,512]{1,0:T(1,128)} %get-tuple-element.47) | copy-start | bytes 6148
  285.6 121.3 %copy-start.51 = (f32[1,512]{1,0:T(1,128)S(1)}, f32[1,512]{1,0:T(1,128)}, u32[]{:S(2)}) copy-start(f32[1,512]{1,0:T(1,128)} %get-tuple-element.46) | copy-start | bytes 6148
  285.7 123.5 %copy-start.55 = (s32[4]{0:T(128)S(1)}, s32[4]{0:T(128)}, u32[]{:S(2)}) copy-start(s32[4]{0:T(128)} %param.9) | copy-start | bytes 52
  285.7 124.8 %copy-start.16 = (bf16[1,394324]{1,0:T(2,128)(2,1)S(1)}, bf16[1,394324]{1,0:T(2,128)(2,1)}, u32[]{:S(2)}) copy-start(bf16[1,394324]{1,0:T(2,128)(2,1)} %copy-done.15) | copy-start | bytes 2365948
  285.7 222.2 %all-gather.8.cloned.1.call-start = ((), (), s32[]{:S(2)}) async-start(), calls=%async_computation.6 | async-start | bytes 7225344 | tf_op jit(solution)/shard_map/all_gather | solution.py:254
  403.8 3.2 copy-start.5
  408.4 200.0 %all-gather.10.cloned.1.call-start = ((), (), s32[]{:S(2)}) async-start(), calls=%async_computation.8 | async-start | bytes 7225344 | tf_op jit(solution)/shard_map/all_gather | solution.py:220
  409.1 330.0 %reduce-scatter.11.cloned.1.call-start = ((), (), s32[]{:S(2)}) async-start(), calls=%async_computation.9 | async-start | bytes 7225344 | tf_op jit(solution)/shard_map/reduce_scatter | solution.py:279
  414.4 100.0 %copy-start.28 = (bf16[512,256]{1,0:T(8,128)(2,1)}, bf16[512,256]{1,0:T(8,128)(2,1)S(1)}, u32[]{:S(2)}) copy-start(bf16[512,256]{1,0:T(8,128)(2,1)S(1)} %squeeze_reshape.22) | copy-start | bytes 786436
  608.4 8.1 copy-start.29
  621.0 240.8 %reduce-scatter.9.cloned.1.call-start = ((), (), s32[]{:S(2)}) async-start(), calls=%async_computation.7 | async-start | bytes 7225344 | tf_op jit(solution)/shard_map/reduce_scatter | solution.py:263
  627.6 234.2 %copy-start.50 = (f32[1,512]{1,0:T(1,128)S(1)}, f32[1,512]{1,0:T(1,128)}, u32[]{:S(2)}) copy-start(f32[1,512]{1,0:T(1,128)} %get-tuple-element.45) | copy-start | bytes 6148
  627.6 339.5 %all-gather.12.cloned.1.call-start = ((), (), s32[]{:S(2)}) async-start(), calls=%async_computation.10 | async-start | bytes 7225344 | tf_op jit(solution)/shard_map/all_gather | solution.py:287
  861.8 5.9 copy-start.40
  861.8 6.6 copy-start.56
  861.8 7.2 copy-start.34
  861.8 7.2 copy-start.37
  867.6 368.0 %reduce-scatter.13.cloned.1.call-start = ((), (), s32[]{:S(2)}) async-start(), calls=%async_computation.11 | async-start | bytes 7225344 | tf_op jit(solution)/shard_map/reduce_scatter | solution.py:300
  878.1 6.2 copy-start.17
  884.3 82.8 %copy-start.30 = (bf16[64,512]{1,0:T(8,128)(2,1)S(1)}, bf16[64,512]{1,0:T(8,128)(2,1)}, u32[]{:S(2)}) copy-start(bf16[64,512]{1,0:T(8,128)(2,1)} %squeeze_reshape.21) | copy-start | bytes 196612
  979.2 8.9 copy-start.19
  979.2 8.9 copy-start.23
  979.2 16.8 %slice-start = ((s8[7340032]{0:T(1024)(128)(4,1)}), s8[3145728]{0:T(1024)(128)(4,1)S(1)}, s32[]{:S(2)}) async-start(s8[7340032]{0:T(1024)(128)(4,1)} %bitcast.149), calls=%async_computation.14 | async-start | bytes 6291456
  988.1 7.9 slice-start.1
  988.1 7.9 copy-start.10
  988.1 7.9 copy-start.11
  1002.0 4.0 copy-start.8
  1006.0 3.2 copy-start.12
  1074.4 4.2 slice-start.2
  1074.9 4.9 slice-start.3
  1074.9 5.3 copy-start.4
  1088.2 5.1 copy-start.26
  1093.3 4.6 copy-start.35
  1093.3 4.6 copy-start.38
  1093.3 4.6 copy-start.44
  1093.3 4.6 copy-start.53
  1117.5 211.8 %all-reduce.8.cloned.1.call-start = ((), (), s32[]{:S(2)}) async-start(), calls=%async_computation.13 | async-start | bytes 3154944
  1142.5 26.1 %copy-start.31 = (f32[1,1,64,512]{3,1,2,0:T(1,128)S(1)}, f32[1,1,64,512]{3,1,2,0:T(1,128)}, u32[]{:S(2)}) copy-start(f32[1,1,64,512]{3,1,2,0:T(1,128)} %copy.126) | copy-start | bytes 393220
  1168.4 69.8 %copy-start.48 = (f32[1,8,64]{2,1,0:T(8,128)S(1)}, f32[1,8,64]{2,1,0:T(8,128)}, u32[]{:S(2)}) copy-start(f32[1,8,64]{2,1,0:T(8,128)} %stack.47) | copy-start | bytes 6148
  1168.4 69.8 %copy-start.46 = (f32[1,8,64]{2,1,0:T(8,128)S(1)}, f32[1,8,64]{2,1,0:T(8,128)}, u32[]{:S(2)}) copy-start(f32[1,8,64]{2,1,0:T(8,128)} %stack.48) | copy-start | bytes 6148
  1168.4 69.8 %copy-start.47 = (f32[1,8,64]{2,1,0:T(8,128)S(1)}, f32[1,8,64]{2,1,0:T(8,128)}, u32[]{:S(2)}) copy-start(f32[1,8,64]{2,1,0:T(8,128)} %stack.49) | copy-start | bytes 6148
  1168.4 69.8 %copy-start.45 = (f32[1,8,64]{2,1,0:T(8,128)S(1)}, f32[1,8,64]{2,1,0:T(8,128)}, u32[]{:S(2)}) copy-start(f32[1,8,64]{2,1,0:T(8,128)} %stack.50) | copy-start | bytes 6148
  1168.4 114.9 %copy-start.54 = (f32[256]{0:T(256)S(1)}, f32[256]{0:T(256)}, u32[]{:S(2)}) copy-start(f32[256]{0:T(256)} %get-tuple-element.59) | copy-start | bytes 3076
  1168.4 121.1 %copy-start.14 = (f32[784,512]{1,0:T(8,128)S(1)}, f32[784,512]{1,0:T(8,128)}, u32[]{:S(2)}) copy-start(f32[784,512]{1,0:T(8,128)} %copy-done.13) | copy-start | bytes 4816900
  1235.7 53.9 %copy-start.20 = (bf16[784,512]{1,0:T(8,128)(2,1)S(1)}, bf16[784,512]{1,0:T(8,128)(2,1)}, u32[]{:S(2)}) copy-start(bf16[784,512]{1,0:T(8,128)(2,1)} %reduce-scatter.13.cloned.1.call-done) | copy-start | bytes 2408452
  1238.0 91.4 %copy-start.27 = (f32[1,98581]{1,0:T(1,128)S(1)}, f32[1,98581]{1,0:T(1,128)}, u32[]{:S(2)}) copy-start(f32[1,98581]{1,0:T(1,128)} %param.10) | copy-start | bytes 1182976
  1238.0 91.4 %copy-start.32 = (f32[1,98581]{1,0:T(1,128)S(1)}, f32[1,98581]{1,0:T(1,128)}, u32[]{:S(2)}) copy-start(f32[1,98581]{1,0:T(1,128)} %param.11) | copy-start | bytes 1182976
  (8 other events, 13.4 us)
Sparse Core Ops, SparseCore 0:
  15.3 37.3 all-reduce.5
  1288.9 40.4 all-reduce.7
Sparse Core Ops, SparseCore 1:
  17.8 103.1 all-gather.5
  285.8 117.9 reduce-scatter.6
  408.4 99.4 all-gather.7
  510.1 98.3 all-gather.9
  621.1 117.9 reduce-scatter.10
  742.7 119.0 reduce-scatter.8
  867.7 99.4 all-gather.11
  1117.6 118.0 reduce-scatter.12
where the time goes:
time: 1350 us; the launch traced here: 1340 us
  waiting for transfers between devices  775 us (57%)
  local copies, waits for them, and re-layouts  298 us (22%)
  matrix products  94.2 us (7%)
  other arithmetic  92.8 us (7%)
  blocking collectives  63.2 us (5%)
  between operations  18.2 us (1%)
    reduce_scatter x1, waiting for transfers between devices, head_block(): lax.psum_scatter(feed_part.astype(jnp.bfloat16), 'mp', scatter_dimension=...  120 us
    reduce_scatter x1, waiting for transfers between devices, head_block(): lax.psum_scatter(partial_value.astype(jnp.bfloat16), 'mp', scatter_dimens...  118 us
    reduce_scatter x1, waiting for transfers between devices, head_block(): lax.psum_scatter(contract_cols(preact_rounded, owner_pieces['fc1_weight']...  111 us
    all_gather x1, waiting for transfers between devices, head_block(): lax.all_gather(cotangent, 'mp', axis=0, tiled=True)  93.9 us
    all_gather x1, waiting for transfers between devices, head_block(): normed2_all = lax.all_gather(normed2, 'mp', axis=0, tiled=True)  93.3 us
    unnamed x154, local copies, waits for them, and re-layouts  79.8 us
    unnamed x12, waiting for transfers between devices  74.9 us
    all_gather x1, waiting for transfers between devices, head_block(): rounded_all = lax.all_gather(residual_rounded, 'mp', axis=0, tiled=True)  73.7 us
  transfers between devices with their start and end apart: 10, of which 10 were waited for; matrix products, arithmetic and copies ran while one was open for 9% of the time, Pallas kernels for 0%

commit v1 on v0

--- a/solution.py
+++ b/solution.py
@@ -251,7 +251,26 @@
     center2, scale2 = norm_stats(residual)
     unit2 = (residual - center2) * scale2
     normed2 = (unit2 * full[3] + full[4]).astype(jnp.bfloat16)
-    normed2_all = lax.all_gather(normed2, "mp", axis=0, tiled=True)
+    count_2, index_2, width_2 = (lax.axis_size("mp"), lax.axis_index("mp"), normed2.shape[0])
+    ahead = [(i, (i + 1) % count_2) for i in range(count_2)]
+    left_2 = [(i, (i - 1) % count_2) for i in range(count_2)]
+    result = jnp.zeros(
+        (*normed2.shape[:0], count_2 * width_2, *normed2.shape[0 + 1 :]), normed2.dtype
+    )
+    result = lax.dynamic_update_slice_in_dim(result, normed2, index_2 * width_2, axis=0)
+    from_left = from_right = normed2
+    halfway = count_2 // 2
+    for step in range(1, halfway + 1):
+        from_left = lax.ppermute(from_left, "mp", ahead)
+        result = lax.dynamic_update_slice_in_dim(
+            result, from_left, (index_2 - step) % count_2 * width_2, axis=0
+        )
+        if step < count_2 - halfway:
+            from_right = lax.ppermute(from_right, "mp", left_2)
+            result = lax.dynamic_update_slice_in_dim(
+                result, from_right, (index_2 + step) % count_2 * width_2, axis=0
+            )
+    normed2_all = result
     hidden_before_gelu = jnp.dot(
         normed2_all, owner_pieces["fc1_weight"][0], preferred_element_type=jnp.float32
     ) + linear_entries_arg("fc1_bias")

time: 1350 us -> 1350 us (level)
  waiting for transfers between devices: 775 us -> 725 us
  starting transfers between devices: 1 us -> 29.9 us
  local copies, waits for them, and re-layouts: 298 us -> 314 us
    ppermute x0 -> x7, waiting for transfers between devices: none -> 135 us  [the longest x4 135 us: head_block(): from_left = lax.ppermute(from_left, 'mp', ahead)]
    all_gather x1, waiting for transfers between devices: 93.9 us -> 0.01 us  [head_block(): lax.all_gather(cotangent, 'mp', axis=0, tiled=True)]
    all_gather x1 -> x0, waiting for transfers between devices: 93.3 us -> none  [head_block(): normed2_all = lax.all_gather(normed2, 'mp', axis=0, tiled=True)]
    ppermute x0 -> x7, starting transfers between devices: none -> 29 us  [the longest x3 20 us: head_block(): from_right = lax.ppermute(from_right, 'mp', left_2)]
    dynamic_update_slice x0 -> x7, local copies, waits for them, and re-layouts: none -> 13.5 us  [the longest x4 7.26 us: head_block(): lax.dynamic_update_slice_in_dim(result, from_left, (index_2 - step) % cou...]
    unnamed x12 -> x11, waiting for transfers between devices: 74.9 us -> 74.8 us
  transfers between devices with their start and end apart: 10 -> 16, of which waited for: 10 -> 12; matrix products, arithmetic and copies ran while one was open for 9% -> 10% of each run, Pallas kernels for 0% -> 0%
where the time goes in v1:
time: 1350 us; the launch traced here: 1340 us
  waiting for transfers between devices  725 us (54%)
  local copies, waits for them, and re-layouts  314 us (23%)
  matrix products  94.3 us (7%)
  other arithmetic  92.9 us (7%)
  blocking collectives  63.1 us (5%)
  starting transfers between devices  29.9 us (2%)
  between operations  18.4 us (1%)
    ppermute x4, waiting for transfers between devices, head_block(): from_left = lax.ppermute(from_left, 'mp', ahead)  135 us
    reduce_scatter x1, waiting for transfers between devices, head_block(): lax.psum_scatter(feed_part.astype(jnp.bfloat16), 'mp', scatter_dimension=...  120 us
    reduce_scatter x1, waiting for transfers between devices, head_block(): lax.psum_scatter(partial_value.astype(jnp.bfloat16), 'mp', scatter_dimens...  117 us
    reduce_scatter x1, waiting for transfers between devices, head_block(): lax.psum_scatter(contract_cols(preact_rounded, owner_pieces['fc1_weight']...  113 us
    unnamed x154, local copies, waits for them, and re-layouts  79.8 us
    unnamed x11, waiting for transfers between devices  74.8 us
    all_gather x1, waiting for transfers between devices, head_block(): rounded_all = lax.all_gather(residual_rounded, 'mp', axis=0, tiled=True)  73.7 us
    reduce_scatter x1, waiting for transfers between devices, head_block(): lax.psum_scatter(norm1_part.astype(jnp.bfloat16), 'mp', scatter_dimension...  63.5 us
  transfers between devices with their start and end apart: 16, of which 12 were waited for; matrix products, arithmetic and copies ran while one was open for 10% of the time, Pallas kernels for 0%

profile of v1, /device:TPU:0, one launch (start us, length us, event | category | flops | bytes accessed | tf_op | source)
XLA Modules:
  0.0 1337.6 jit_solution(15934537453444347148)
XLA Ops:
  16.1 36.5 %all-reduce.6.cloned.1.call-done = bf16[394324]{0:T(1024)(128)(2,1)} async-done(((bf16[394324]{0:T(1024)(128)(2,1)}), bf16[394324]{0:T(1024)(128)(2,1)}) %all-reduce.6.cloned.1.call-update) | async-done | bytes 788664
  52.6 8.4 reshape.473
  61.5 27.7 %all-gather = bf16[8,64,6]{1,2,0:T(8,128)(2,1)S(1)} all-gather(bf16[1,64,6]{1,2,0:T(8,128)(2,1)S(1)} %bitcast.188), channel_id=1, replica_groups=mesh['dp'=4,'mp'=8] {'mp'}, dimensions={0}, use_global_device_ids=true | all-gather | bytes 6912 | tf_op jit(solution)/shard_map/all_gather | solution.py:221
  93.6 27.4 %all-gather.5.cloned.1.call-done = bf16[6272,512]{1,0:T(8,128)(2,1)} async-done(((bf16[784,512]{1,0:T(8,128)(2,1)}), bf16[6272,512]{1,0:T(8,128)(2,1)}) %all-gather.5.cloned.1.call-update) | async-done | bytes 6422544 | tf_op jit(solution)/shard_map/all_gather | solution.py:219
  121.0 3.9 convert_reduce_fusion
  125.6 2.9 fusion.2
  128.6 5.8 fusion.4
  134.4 12.6 copy.83
  147.0 21.8 %reshape_reshape.20 = bf16[32,14,14,192]{3,2,1,0:T(8,128)(2,1)} reshape(bf16[6272,2,3,32]{3,2,1,0:T(4,128)(2,1)} %copy.83) | data formatting | bytes 4816896 | tf_op jit(solution)/shard_map/reshape;reshape | solution.py:111
  177.0 11.2 reshape_reshape.21
  188.2 25.3 %fusion.109 = (bf16[32,4,49,2,1,32]{5,4,3,0,2,1:T(2,128)(2,1)}, bf16[32,4,49,2,1,32]{5,4,3,0,2,1:T(2,128)(2,1)}, bf16[32,4,49,2,1,32]{5,4,3,0,2,1:T(2,128)(2,1)}) fusion(bf16[32,4,49,2,3,32]{5,4,3,0,2,1:T(4,128)(2,1)} %reshape_reshape.21), kind=kLoop, calls=%fused_computation.217 | loop fusion | bytes 4816896 | tf_op jit(solution)/shard_map/slice | solution.py:164
  213.5 12.7 copy.124
  226.2 14.0 %copy.123 = bf16[32,4,49,2,1,32]{2,5,3,1,0,4:T(8,128)(2,1)} copy(bf16[32,4,49,2,1,32]{5,4,3,0,2,1:T(2,128)(2,1)} %get-tuple-element.31) | data formatting | bytes 1605632
  240.2 14.1 %copy.125 = bf16[32,4,49,2,1,32]{2,5,3,1,0,4:T(8,128)(2,1)} copy(bf16[32,4,49,2,1,32]{5,4,3,0,2,1:T(2,128)(2,1)} %get-tuple-element.32) | data formatting | bytes 1605632
  254.4 3.8 fusion.18
  261.5 3.4 convert_bitcast_fusion
  264.9 7.8 copy.92
  280.4 5.4 convolution_convert_fusion.3
  286.7 117.3 %reduce-scatter.7.cloned.1.call-done = bf16[784,512]{1,0:T(8,128)(2,1)} async-done(((bf16[6272,512]{1,0:T(8,128)(2,1)}), bf16[784,512]{1,0:T(8,128)(2,1)}) %reduce-scatter.7.cloned.1.call-update) | async-done | bytes 802832 | tf_op jit(solution)/shard_map/reduce_scatter | solution.py:244
  407.2 3.1 broadcast_in_dim.19
  413.2 3.2 collective-permute-start.1
  416.5 38.9 %collective-permute-done = bf16[784,512]{1,0:T(8,128)(2,1)S(1)} collective-permute-done((bf16[784,512]{1,0:T(8,128)(2,1)S(1)}, bf16[784,512]{1,0:T(8,128)(2,1)S(1)}, u32[]{:S(2)}, u32[]{:S(2)}) %collective-permute-start) | collective-permute-done | bytes 802848 | tf_op jit(solution)/shard_map/ppermute | solution.py:264
  460.1 47.2 %collective-permute-done.2 = bf16[784,512]{1,0:T(8,128)(2,1)} collective-permute-done((bf16[784,512]{1,0:T(8,128)(2,1)S(1)}, bf16[784,512]{1,0:T(8,128)(2,1)}, u32[]{:S(2)}, u32[]{:S(2)}) %collective-permute-start.2) | collective-permute-done | bytes 802848 | tf_op jit(solution)/shard_map/ppermute | solution.py:264
  511.2 3.0 slice_reduce_fusion.2
  514.2 14.5 %collective-permute-start.5 = (bf16[784,512]{1,0:T(8,128)(2,1)}, bf16[784,512]{1,0:T(8,128)(2,1)}, u32[]{:S(2)}, u32[]{:S(2)}) collective-permute-start(bf16[784,512]{1,0:T(8,128)(2,1)} %collective-permute-done.3), channel_id=1, source_target_pairs={{0,7},{1,0},{2,1},{3,2},{4,3},{5,4},{6,5},{7,6},{8,15},{9,8},{10,9... | collective-permute-start | bytes 2408456 | tf_op jit(solution)/shard_map/ppermute | solution.py:269
  528.7 30.7 %collective-permute-done.4 = bf16[784,512]{1,0:T(8,128)(2,1)} collective-permute-done((bf16[784,512]{1,0:T(8,128)(2,1)}, bf16[784,512]{1,0:T(8,128)(2,1)}, u32[]{:S(2)}, u32[]{:S(2)}) %collective-permute-start.4) | collective-permute-done | bytes 802848 | tf_op jit(solution)/shard_map/ppermute | solution.py:264
  574.4 18.3 %collective-permute-done.6 = bf16[784,512]{1,0:T(8,128)(2,1)} collective-permute-done((bf16[784,512]{1,0:T(8,128)(2,1)}, bf16[784,512]{1,0:T(8,128)(2,1)}, u32[]{:S(2)}, u32[]{:S(2)}) %collective-permute-start.6) | collective-permute-done | bytes 802848 | tf_op jit(solution)/shard_map/ppermute | solution.py:264
  594.7 6.6 multiply_convert_fusion
  601.3 8.0 fusion.113
  609.3 4.6 convolution_convert_fusion.1
  614.4 6.4 convolution_convert_fusion.2
  621.5 113.1 %reduce-scatter.11.cloned.1.call-done = bf16[784,512]{1,0:T(8,128)(2,1)} async-done(((bf16[6272,512]{1,0:T(8,128)(2,1)}), bf16[784,512]{1,0:T(8,128)(2,1)}) %reduce-scatter.11.cloned.1.call-update) | async-done | bytes 802832 | tf_op jit(solution)/shard_map/reduce_scatter | solution.py:298
  734.7 2.7 fusion.57
  737.4 120.0 %reduce-scatter.9.cloned.1.call-done = bf16[784,512]{1,0:T(8,128)(2,1)} async-done(((bf16[6272,512]{1,0:T(8,128)(2,1)}), bf16[784,512]{1,0:T(8,128)(2,1)}) %reduce-scatter.9.cloned.1.call-update) | async-done | bytes 802832 | tf_op jit(solution)/shard_map/reduce_scatter | solution.py:282
  857.4 3.6 fusion.107
  864.6 9.1 fusion
  873.7 4.9 fusion.65
  879.9 5.1 fusion.68
  889.0 73.7 %all-gather.9.cloned.1.call-done = bf16[6272,512]{1,0:T(8,128)(2,1)} async-done(((bf16[784,512]{1,0:T(8,128)(2,1)}), bf16[6272,512]{1,0:T(8,128)(2,1)}) %all-gather.9.cloned.1.call-update) | async-done | bytes 6422544 | tf_op jit(solution)/shard_map/all_gather | solution.py:306
  962.7 4.9 convolution_convert_fusion.4
  971.9 2.9 reshape_reshape.23
  974.8 8.8 copy.98
  983.6 7.9 convolution_bitcast_fusion
  991.6 3.2 multiply_reduce_fusion
  994.8 2.8 fusion.106
  997.6 4.0 convolution_bitcast_fusion.1
  1001.5 3.2 multiply_bitcast_fusion
  1004.7 10.6 pad_maximum_fusion
  1015.3 23.6 %copy.103 = f32[32,4,49,2,3,32]{5,4,3,0,2,1:T(4,128)} copy(f32[32,4,49,2,3,32]{2,5,3,1,0,4:T(8,128)} %pad_maximum_fusion) | data formatting | bytes 9633792 | tf_op jit(solution)/shard_map/stack | solution.py:201
  1038.9 26.7 %reshape_reshape.24 = f32[32,2,2,7,7,192]{5,0,4,3,2,1:T(8,128)} reshape(f32[32,4,49,2,3,32]{5,4,3,0,2,1:T(4,128)} %copy.103) | data formatting | bytes 9633792 | tf_op jit(solution)/shard_map/reshape;reshape | solution.py:120
  1065.6 3.4 copy.104
  1070.4 3.7 fusion.10
  1080.0 3.7 copy.105
  1083.7 5.1 convert_element_type.224
  1088.8 4.6 convolution_convert_fusion
  1093.4 8.6 fusion.47
  1103.5 9.5 copy.107
  1113.1 24.9 %reshape_reshape.25 = f32[6272,2,3,32]{3,2,1,0:T(4,128)} reshape(f32[32,14,14,192]{3,2,1,0:T(8,128)} %copy.107) | data formatting | bytes 9633792 | tf_op jit(solution)/shard_map/reshape;reshape | solution.py:312
  1138.0 25.9 %slice_reduce_fusion = (f32[2,32]{1,0:T(2,128)S(1)}, f32[2,32]{1,0:T(2,128)S(1)}) fusion(f32[6272,2,3,32]{3,2,1,0:T(4,128)} %reshape_reshape.25), kind=kLoop, calls=%fused_computation.27 | loop fusion | flops 802688 | bytes 3211776 | tf_op jit(solution)/shard_map/reduce_sum | solution.py:314
  1167.7 63.5 %reduce-scatter.13.cloned.1.call-done = bf16[784,512]{1,0:T(8,128)(2,1)} async-done(((bf16[6272,512]{1,0:T(8,128)(2,1)}), bf16[784,512]{1,0:T(8,128)(2,1)}) %reduce-scatter.13.cloned.1.call-update) | async-done | bytes 802832 | tf_op jit(solution)/shard_map/reduce_scatter | solution.py:319
  1233.7 35.5 %all-reduce.1 = f32[6,8,64]{2,1,0:T(8,128)S(1)} all-reduce(f32[6,8,64]{2,1,0:T(8,128)S(1)} %constant_dynamic-update-slice_fusion), channel_id=6, replica_groups=mesh['dp'=4,'mp'=8] {'mp'}, use_global_device_ids=true, to_apply=%region_22.23.clone | all-reduce | flops 3072 | bytes 24576
  1284.9 2.8 fusion.51
  1287.7 37.1 %all-reduce.8.cloned.1.call-done = f32[1,394324]{1,0:T(1,128)} async-done(((f32[1,394324]{1,0:T(1,128)}), f32[1,394324]{1,0:T(1,128)}) %all-reduce.8.cloned.1.call-update) | async-done | bytes 1577312
  1324.8 4.9 multiply_subtract_fusion
  (277 shorter events, 109.2 us)
Async XLA Ops:
  8.0 44.7 %all-reduce.6.cloned.1.call-start = ((), (), s32[]{:S(2)}) async-start(), calls=%async_computation.11 | async-start | bytes 1581056
  15.1 105.8 %all-gather.5.cloned.1.call-start = ((), (), s32[]{:S(2)}) async-start(), calls=%async_computation.4 | async-start | bytes 7225344 | tf_op jit(solution)/shard_map/all_gather | solution.py:219
  15.7 388.3 %reduce-scatter.7.cloned.1.call-start = ((), (), s32[]{:S(2)}) async-start(), calls=%async_computation.5 | async-start | bytes 7225344 | tf_op jit(solution)/shard_map/reduce_scatter | solution.py:244
  16.0 75.5 %copy-start.39 = (s32[49,49]{1,0:T(8,128)}, s32[49,49]{1,0:T(8,128)S(1)}, u32[]{:S(2)}) copy-start(s32[49,49]{1,0:T(8,128)S(1)} %add_add_fusion.2) | copy-start | bytes 28816
  61.0 63.9 %copy-start.15 = (bf16[1,394324]{1,0:T(2,128)(2,1)}, bf16[1,394324]{1,0:T(2,128)(2,1)S(1)}, u32[]{:S(2)}) copy-start(bf16[1,394324]{1,0:T(2,128)(2,1)S(1)} %reshape.473) | copy-start | bytes 2365948
  90.5 170.4 %copy-start.22 = (f32[2,49,49]{1,2,0:T(8,128)}, f32[2,49,49]{1,2,0:T(8,128)S(1)}, u32[]{:S(2)}) copy-start(f32[2,49,49]{1,2,0:T(8,128)S(1)} %copy.90) | copy-start | bytes 57628
  92.8 35.7 %copy-start.25 = (bf16[512,192]{1,0:T(8,128)(2,1)}, bf16[512,192]{1,0:T(8,128)(2,1)S(1)}, u32[]{:S(2)}) copy-start(bf16[512,192]{1,0:T(8,128)(2,1)S(1)} %squeeze_reshape.19) | copy-start | bytes 589828
  93.6 35.0 %copy-start.43 = (f32[1,512]{1,0:T(1,128)}, f32[1,512]{1,0:T(1,128)S(1)}, u32[]{:S(2)}) copy-start(f32[1,512]{1,0:T(1,128)S(1)} %get-tuple-element.52) | copy-start | bytes 6148
  93.6 35.0 %copy-start.52 = (f32[1,512]{1,0:T(1,128)}, f32[1,512]{1,0:T(1,128)S(1)}, u32[]{:S(2)}) copy-start(f32[1,512]{1,0:T(1,128)S(1)} %get-tuple-element.51) | copy-start | bytes 6148
  121.0 4.7 copy-start.1
  125.6 8.8 copy-start.33
  128.6 5.8 copy-start.36
  226.2 28.1 %copy-start.6 = (bf16[32,4,49,2,1,32]{2,5,3,1,0,4:T(8,128)(2,1)}, bf16[32,4,49,2,1,32]{2,5,3,1,0,4:T(8,128)(2,1)S(1)}, u32[]{:S(2)}) copy-start(bf16[32,4,49,2,1,32]{2,5,3,1,0,4:T(8,128)(2,1)S(1)} %copy.124) | copy-start | bytes 2408452
  285.8 118.2 %copy-start.2 = (bf16[784,512]{1,0:T(8,128)(2,1)S(1)}, bf16[784,512]{1,0:T(8,128)(2,1)}, u32[]{:S(2)}) copy-start(bf16[784,512]{1,0:T(8,128)(2,1)} %param.7) | copy-start | bytes 2408452
  285.8 118.2 %copy-start.41 = (f32[1,512]{1,0:T(1,128)S(1)}, f32[1,512]{1,0:T(1,128)}, u32[]{:S(2)}) copy-start(f32[1,512]{1,0:T(1,128)} %get-tuple-element.50) | copy-start | bytes 6148
  285.9 315.4 %all-gather.7.cloned.1.call-start = ((), (), s32[]{:S(2)}) async-start(), calls=%async_computation.7 | async-start | bytes 7225344 | tf_op jit(solution)/shard_map/all_gather | solution.py:220
  286.4 448.2 %reduce-scatter.11.cloned.1.call-start = ((), (), s32[]{:S(2)}) async-start(), calls=%async_computation.8 | async-start | bytes 7225344 | tf_op jit(solution)/shard_map/reduce_scatter | solution.py:298
  405.5 4.8 copy-start.5
  405.5 4.8 copy-start.42
  405.5 4.8 copy-start.51
  407.2 102.7 %copy-start.55 = (s32[4]{0:T(128)S(1)}, s32[4]{0:T(128)}, u32[]{:S(2)}) copy-start(s32[4]{0:T(128)} %param.9) | copy-start | bytes 52
  407.2 104.0 %copy-start.16 = (bf16[1,394324]{1,0:T(2,128)(2,1)S(1)}, bf16[1,394324]{1,0:T(2,128)(2,1)}, u32[]{:S(2)}) copy-start(bf16[1,394324]{1,0:T(2,128)(2,1)} %copy-done.15) | copy-start | bytes 2365948
  411.7 43.6 %collective-permute-start = (bf16[784,512]{1,0:T(8,128)(2,1)S(1)}, bf16[784,512]{1,0:T(8,128)(2,1)S(1)}, u32[]{:S(2)}, u32[]{:S(2)}) collective-permute-start(bf16[784,512]{1,0:T(8,128)(2,1)S(1)} %get-tuple-element.29), channel_id=1, source_target_pairs={{0,1},{1,2},{2,3},{3,4},{4,5},{5,6},{6,7},{7,0},{8,9},{9,10},{10,1... | collective-permute-start | bytes 2408456 | tf_op jit(solution)/shard_map/ppermute | solution.py:264
  413.2 44.6 %collective-permute-start.1 = (bf16[784,512]{1,0:T(8,128)(2,1)S(1)}, bf16[784,512]{1,0:T(8,128)(2,1)}, u32[]{:S(2)}, u32[]{:S(2)}) collective-permute-start(bf16[784,512]{1,0:T(8,128)(2,1)S(1)} %get-tuple-element.29), channel_id=1, source_target_pairs={{0,7},{1,0},{2,1},{3,2},{4,3},{5,4},{6,5},{7,6},{8,15},{9,8},{10,9... | collective-permute-start | bytes 2408456 | tf_op jit(solution)/shard_map/ppermute | solution.py:269
  455.3 52.0 %collective-permute-start.2 = (bf16[784,512]{1,0:T(8,128)(2,1)S(1)}, bf16[784,512]{1,0:T(8,128)(2,1)}, u32[]{:S(2)}, u32[]{:S(2)}) collective-permute-start(bf16[784,512]{1,0:T(8,128)(2,1)S(1)} %collective-permute-done), channel_id=1, source_target_pairs={{0,1},{1,2},{2,3},{3,4},{4,5},{5,6},{6,7},{7,0},{8,9},{9,10},{10,1... | collective-permute-start | bytes 2408456 | tf_op jit(solution)/shard_map/ppermute | solution.py:264
  457.8 56.4 %collective-permute-start.3 = (bf16[784,512]{1,0:T(8,128)(2,1)}, bf16[784,512]{1,0:T(8,128)(2,1)}, u32[]{:S(2)}, u32[]{:S(2)}) collective-permute-start(bf16[784,512]{1,0:T(8,128)(2,1)} %collective-permute-done.1), channel_id=1, source_target_pairs={{0,7},{1,0},{2,1},{3,2},{4,3},{5,4},{6,5},{7,6},{8,15},{9,8},{10,9... | collective-permute-start | bytes 2408456 | tf_op jit(solution)/shard_map/ppermute | solution.py:269
  507.3 52.1 %collective-permute-start.4 = (bf16[784,512]{1,0:T(8,128)(2,1)}, bf16[784,512]{1,0:T(8,128)(2,1)}, u32[]{:S(2)}, u32[]{:S(2)}) collective-permute-start(bf16[784,512]{1,0:T(8,128)(2,1)} %collective-permute-done.2), channel_id=1, source_target_pairs={{0,1},{1,2},{2,3},{3,4},{4,5},{5,6},{6,7},{7,0},{8,9},{9,10},{10,1... | collective-permute-start | bytes 2408456 | tf_op jit(solution)/shard_map/ppermute | solution.py:264
  514.2 58.1 %collective-permute-start.5 = (bf16[784,512]{1,0:T(8,128)(2,1)}, bf16[784,512]{1,0:T(8,128)(2,1)}, u32[]{:S(2)}, u32[]{:S(2)}) collective-permute-start(bf16[784,512]{1,0:T(8,128)(2,1)} %collective-permute-done.3), channel_id=1, source_target_pairs={{0,7},{1,0},{2,1},{3,2},{4,3},{5,4},{6,5},{7,6},{8,15},{9,8},{10,9... | collective-permute-start | bytes 2408456 | tf_op jit(solution)/shard_map/ppermute | solution.py:269
  559.4 33.2 %collective-permute-start.6 = (bf16[784,512]{1,0:T(8,128)(2,1)}, bf16[784,512]{1,0:T(8,128)(2,1)}, u32[]{:S(2)}, u32[]{:S(2)}) collective-permute-start(bf16[784,512]{1,0:T(8,128)(2,1)} %collective-permute-done.4), channel_id=1, source_target_pairs={{0,1},{1,2},{2,3},{3,4},{4,5},{5,6},{6,7},{7,0},{8,9},{9,10},{10,1... | collective-permute-start | bytes 2408456 | tf_op jit(solution)/shard_map/ppermute | solution.py:264
  562.9 31.8 %copy-start.28 = (bf16[512,256]{1,0:T(8,128)(2,1)}, bf16[512,256]{1,0:T(8,128)(2,1)S(1)}, u32[]{:S(2)}) copy-start(bf16[512,256]{1,0:T(8,128)(2,1)S(1)} %squeeze_reshape.22) | copy-start | bytes 786436
  601.3 8.0 copy-start.29
  614.0 243.4 %reduce-scatter.9.cloned.1.call-start = ((), (), s32[]{:S(2)}) async-start(), calls=%async_computation.6 | async-start | bytes 7225344 | tf_op jit(solution)/shard_map/reduce_scatter | solution.py:282
  620.8 236.6 %copy-start.50 = (f32[1,512]{1,0:T(1,128)S(1)}, f32[1,512]{1,0:T(1,128)}, u32[]{:S(2)}) copy-start(f32[1,512]{1,0:T(1,128)} %get-tuple-element.47) | copy-start | bytes 6148
  620.8 341.9 %all-gather.9.cloned.1.call-start = ((), (), s32[]{:S(2)}) async-start(), calls=%async_computation.9 | async-start | bytes 7225344 | tf_op jit(solution)/shard_map/all_gather | solution.py:306
  857.4 5.8 copy-start.40
  857.4 6.6 copy-start.56
  857.4 7.2 copy-start.34
  857.4 7.2 copy-start.37
  863.2 367.9 %reduce-scatter.13.cloned.1.call-start = ((), (), s32[]{:S(2)}) async-start(), calls=%async_computation.10 | async-start | bytes 7225344 | tf_op jit(solution)/shard_map/reduce_scatter | solution.py:319
  873.7 6.2 copy-start.17
  879.9 82.8 %copy-start.30 = (bf16[64,512]{1,0:T(8,128)(2,1)S(1)}, bf16[64,512]{1,0:T(8,128)(2,1)}, u32[]{:S(2)}) copy-start(bf16[64,512]{1,0:T(8,128)(2,1)} %squeeze_reshape.21) | copy-start | bytes 196612
  974.8 8.8 copy-start.19
  974.8 8.8 copy-start.23
  974.8 16.7 %slice-start = ((s8[7340032]{0:T(1024)(128)(4,1)}), s8[3145728]{0:T(1024)(128)(4,1)S(1)}, s32[]{:S(2)}) async-start(s8[7340032]{0:T(1024)(128)(4,1)} %bitcast.149), calls=%async_computation.13 | async-start | bytes 6291456
  983.6 7.9 slice-start.1
  983.6 7.9 copy-start.10
  983.6 7.9 copy-start.11
  1070.3 4.9 slice-start.3
  1070.3 5.3 copy-start.4
  1083.7 5.1 copy-start.26
  1088.8 4.6 copy-start.35
  1088.8 4.6 copy-start.38
  1088.8 4.6 copy-start.44
  1113.1 211.7 %all-reduce.8.cloned.1.call-start = ((), (), s32[]{:S(2)}) async-start(), calls=%async_computation.12 | async-start | bytes 3154944
  1138.0 26.1 %copy-start.31 = (f32[1,1,64,512]{3,1,2,0:T(1,128)S(1)}, f32[1,1,64,512]{3,1,2,0:T(1,128)}, u32[]{:S(2)}) copy-start(f32[1,1,64,512]{3,1,2,0:T(1,128)} %copy.126) | copy-start | bytes 393220
  1163.9 69.8 %copy-start.48 = (f32[1,8,64]{2,1,0:T(8,128)S(1)}, f32[1,8,64]{2,1,0:T(8,128)}, u32[]{:S(2)}) copy-start(f32[1,8,64]{2,1,0:T(8,128)} %stack.47) | copy-start | bytes 6148
  1163.9 69.7 %copy-start.46 = (f32[1,8,64]{2,1,0:T(8,128)S(1)}, f32[1,8,64]{2,1,0:T(8,128)}, u32[]{:S(2)}) copy-start(f32[1,8,64]{2,1,0:T(8,128)} %stack.48) | copy-start | bytes 6148
  1163.9 69.8 %copy-start.47 = (f32[1,8,64]{2,1,0:T(8,128)S(1)}, f32[1,8,64]{2,1,0:T(8,128)}, u32[]{:S(2)}) copy-start(f32[1,8,64]{2,1,0:T(8,128)} %stack.49) | copy-start | bytes 6148
  1163.9 69.8 %copy-start.45 = (f32[1,8,64]{2,1,0:T(8,128)S(1)}, f32[1,8,64]{2,1,0:T(8,128)}, u32[]{:S(2)}) copy-start(f32[1,8,64]{2,1,0:T(8,128)} %stack.50) | copy-start | bytes 6148
  1163.9 115.0 %copy-start.54 = (f32[256]{0:T(256)S(1)}, f32[256]{0:T(256)}, u32[]{:S(2)}) copy-start(f32[256]{0:T(256)} %get-tuple-element.61) | copy-start | bytes 3076
  1163.9 121.0 %copy-start.14 = (f32[784,512]{1,0:T(8,128)S(1)}, f32[784,512]{1,0:T(8,128)}, u32[]{:S(2)}) copy-start(f32[784,512]{1,0:T(8,128)} %copy-done.13) | copy-start | bytes 4816900
  1231.1 53.8 %copy-start.20 = (bf16[784,512]{1,0:T(8,128)(2,1)S(1)}, bf16[784,512]{1,0:T(8,128)(2,1)}, u32[]{:S(2)}) copy-start(bf16[784,512]{1,0:T(8,128)(2,1)} %reduce-scatter.13.cloned.1.call-done) | copy-start | bytes 2408452
  1233.5 91.3 %copy-start.27 = (f32[1,98581]{1,0:T(1,128)S(1)}, f32[1,98581]{1,0:T(1,128)}, u32[]{:S(2)}) copy-start(f32[1,98581]{1,0:T(1,128)} %param.10) | copy-start | bytes 1182976
  1233.5 91.3 %copy-start.32 = (f32[1,98581]{1,0:T(1,128)S(1)}, f32[1,98581]{1,0:T(1,128)}, u32[]{:S(2)}) copy-start(f32[1,98581]{1,0:T(1,128)} %param.11) | copy-start | bytes 1182976
  (14 other events, 36.4 us)
Sparse Core Ops, SparseCore 0:
  15.3 37.3 all-reduce.5
  1284.3 40.4 all-reduce.7
Sparse Core Ops, SparseCore 1:
  17.8 103.1 all-gather.4
  285.9 118.0 reduce-scatter.6
  406.1 186.8 all-gather.6
  614.1 120.5 reduce-scatter.10
  738.3 119.0 reduce-scatter.8
  863.3 99.4 all-gather.8
  1113.2 117.9 reduce-scatter.12
